TPU v7x, 32 devices: a whole 2x2x4 slice. The times are simulated.
32 devices in a mesh: rows: 8 (over z, x), cols: 4 (over y, core).
Axes of the slice: x: 2, y: 2, z: 4, core: 2. Of those that a mesh axis runs over, the one named last changes fastest.
Arguments:
- basis: float32 [8192, 4096], P('rows', 'cols'), may hold values from -119.66257 to 119.66257, as said below
- block: float32 [8192, 512], P('rows', 'cols'), may hold values from -1800 to 1800
Outputs:
- ortho: float32 [8192, 512], P('rows', 'cols')
- factors: float32 [4, 128, 128], P('cols')
Inputs may be any that keep to these rules, and one draw needn't show every extreme that they name: Under the inner product (sum over rows divided by 8192) the basis columns have squared norms between 0.6 and 1.9, and inner products of distinct basis columns are at most 0.05 in magnitude.
All inputs are finite; a program needn't handle non-finite values.
Results may differ from a plain program's by a relative error of at most 0.000076.
Values sent between devices are 32-bit elements; how exact they have to be, the bound alone decides.
No kernel may reach another device: no remote copies, remote signals or barrier semaphores. Data moves between devices by JAX's collectives and lax.ppermute only.
A program may use at most 64 MiB of HBM per device.

v0:
```python
import jax
import jax.numpy as jnp
from jax import lax
from jax.sharding import PartitionSpec as P

BLK = 128


def solve_block(lower_factor, vectors):
    return jax.scipy.linalg.solve_triangular(lower_factor, vectors, lower=True)


def body(basis, block):
    highest = lax.Precision.HIGHEST
    local_rows = basis.shape[0]
    inverse = 1.0 / (local_rows * lax.axis_size("rows"))
    width = block.shape[1]
    column_index = lax.axis_index("cols")

    def project(piece):
        return (
            lax.dot_general(
                basis,
                piece,
                (((0,), (0,)), ((), ())),
                precision=highest,
                preferred_element_type=jnp.float32,
            )
            * inverse
        )

    def expand(coef):
        return jnp.dot(basis, coef, precision=highest, preferred_element_type=jnp.float32)

    terms_one = project(lax.all_gather(block, "cols", axis=1, tiled=True))
    coef_one = lax.psum(terms_one, "rows")
    placed = lax.dynamic_update_slice_in_dim(
        jnp.zeros((local_rows, coef_one.shape[1]), jnp.float32), block, column_index * width, 1
    )
    first_whole = lax.psum(placed - expand(coef_one), "cols")
    terms_two = project(first_whole)
    first = lax.dynamic_slice_in_dim(first_whole, column_index * width, width, 1)
    coef_two = lax.psum(terms_two, "rows")
    second = first - lax.psum_scatter(expand(coef_two), "cols", scatter_dimension=1, tiled=True)
    blocks = width // BLK
    pieces = second.reshape(local_rows, blocks, BLK)
    gram = jnp.einsum("mbi,mbj->bij", pieces, pieces, precision=highest) * inverse
    gram = lax.psum(gram, "rows")
    lower_factor = jnp.linalg.cholesky(gram)
    solved = jax.vmap(solve_block)(lower_factor, jnp.transpose(pieces, (1, 2, 0)))
    ortho = jnp.transpose(solved, (2, 0, 1)).reshape(local_rows, width)
    return (ortho, jnp.transpose(lower_factor, (0, 2, 1)))


def solution(mesh):
    placed = (P("rows", "cols"), P("rows", "cols"))
    return jax.shard_map(
        body,
        mesh=mesh,
        in_specs=placed,
        out_specs=(P("rows", "cols"), P("cols", None, None)),
        check_vma=False,
    )
```

profile of v0, /device:TPU:0, one launch (start us, length us, event | category | flops | bytes accessed | tf_op | source)
XLA Modules:
  0.0 476.0 jit_solution(7517272405939530119)
XLA Ops:
  7.2 0.0 all-gather.2.cloned.1.call-start
  7.2 0.7 all-gather.2.cloned.1.call-update
  7.9 0.0 all-reduce.5.cloned.1.call-start
  7.9 27.2 %all-gather.2.cloned.1.call-done = f32[1024,512]{1,0:T(8,128)} async-done(((f32[1024,128]{1,0:T(8,128)}), f32[1024,512]{1,0:T(8,128)}) %all-gather.2.cloned.1.call-update) | async-done | bytes 2097168 | tf_op jit(solution)/shard_map/all_gather | solution.py:35
  35.1 10.2 %convolution_multiply_fusion = f32[1024,512]{1,0:T(8,128)} fusion(f32[1024,1024]{1,0:T(8,128)} %param.2, f32[1024,512]{1,0:T(8,128)} %all-gather.2.cloned.1.call-done), kind=kOutput, calls=%fused_computation.3 | convolution fusion | flops 6442975232 | bytes 8388608 | tf_op jit(solution)/shard_map/dot_general | solution.py:22
  45.3 0.0 copy-start.1
  45.3 0.0 all-reduce.5.cloned.1.call-update
  45.3 0.0 all-reduce.7.cloned.1.call-start
  45.4 1.0 copy-done.1
  46.3 0.2 copy.4
  46.5 0.2 broadcast_in_dim.7
  46.8 0.1 constant_dynamic-update-slice_fusion
  46.8 100.9 %all-reduce.5.cloned.1.call-done = f32[1024,512]{1,0:T(8,128)} async-done(((f32[1024,512]{1,0:T(8,128)}), f32[1024,512]{1,0:T(8,128)}) %all-reduce.5.cloned.1.call-update) | async-done | bytes 2097168 | tf_op jit(solution)/shard_map/psum | solution.py:36
  147.8 16.7 %bitcast_subtract_fusion = f32[1024,512]{0,1:T(8,128)} fusion(f32[1024,512]{0,1:T(8,128)S(1)} %constant_dynamic-update-slice_fusion, f32[1024,512]{1,0:T(8,128)} %all-reduce.5.cloned.1.call-done, f32[1024,1024]{1,0:T(8,128)} %param.2), kind=kOutput, calls=%fused_computation | convolution fusion | flops 6442975232 | bytes 10485760 | tf_op jit(solution)/shard_map/dot_general | solution.py:33
  164.5 0.0 all-reduce.7.cloned.1.call-update
  164.5 0.2 all-reduce.9.cloned.1.call-start
  164.7 50.6 %all-reduce.7.cloned.1.call-done = f32[1024,512]{0,1:T(8,128)} async-done(((f32[1024,512]{0,1:T(8,128)}), f32[1024,512]{0,1:T(8,128)}) %all-reduce.7.cloned.1.call-update) | async-done | bytes 2097168 | tf_op jit(solution)/shard_map/psum | solution.py:40
  215.3 10.2 %multiply_bitcast_fusion = f32[1024,512]{0,1:T(8,128)} fusion(f32[1024,512]{0,1:T(8,128)} %all-reduce.7.cloned.1.call-done, f32[1024,1024]{1,0:T(8,128)} %param.2), kind=kOutput, calls=%fused_computation.1 | convolution fusion | flops 6442975232 | bytes 8388608 | tf_op jit(solution)/shard_map/dot_general | solution.py:22
  225.6 0.0 all-reduce.9.cloned.1.call-update
  225.6 0.0 reduce-scatter.2.cloned.1.call-start
  225.6 102.5 %all-reduce.9.cloned.1.call-done = f32[1024,512]{0,1:T(8,128)} async-done(((f32[1024,512]{0,1:T(8,128)}), f32[1024,512]{0,1:T(8,128)}) %all-reduce.9.cloned.1.call-update) | async-done | bytes 2097168 | tf_op jit(solution)/shard_map/psum | solution.py:43
  328.1 10.3 %convolution_bitcast_fusion = f32[1024,512]{0,1:T(8,128)} fusion(f32[1024,512]{0,1:T(8,128)} %all-reduce.9.cloned.1.call-done, f32[1024,1024]{1,0:T(8,128)} %param.2), kind=kOutput, calls=%fused_computation.2 | convolution fusion | flops 6442450944 | bytes 8388608 | tf_op jit(solution)/shard_map/dot_general | solution.py:33
  338.4 0.0 copy-start
  338.4 0.0 reduce-scatter.2.cloned.1.call-update
  338.4 0.3 all-reduce.11.cloned.1.call-start
  338.7 30.3 %reduce-scatter.2.cloned.1.call-done = f32[1024,128]{0,1:T(8,128)} async-done(((f32[1024,512]{0,1:T(8,128)}), f32[1024,128]{0,1:T(8,128)}) %reduce-scatter.2.cloned.1.call-update) | async-done | bytes 524304 | tf_op jit(solution)/shard_map/reduce_scatter | solution.py:44
  369.0 0.0 copy-done
  369.0 0.0 copy-start.2
  369.0 2.5 fusion
  371.5 0.0 all-reduce.11.cloned.1.call-update
  371.5 70.6 %all-reduce.11.cloned.1.call-done = f32[1,128,128]{1,2,0:T(8,128)} async-done(((f32[1,128,128]{1,2,0:T(8,128)}), f32[1,128,128]{1,2,0:T(8,128)}) %all-reduce.11.cloned.1.call-update) | async-done | bytes 65552 | tf_op jit(solution)/shard_map/psum | solution.py:48
  442.2 0.9 copy.6
  443.1 0.9 fusion.3
  444.0 11.7 %custom-call.8 = f32[1,128,128]{2,1,0:T(8,128)S(1)} custom-call(f32[1,128,128]{2,1,0:T(8,128)S(1)} %fusion.3), custom_call_target="Cholesky" | custom-call | tf_op jit(solution)/shard_map/jit(cholesky)/cholesky | solution.py:49
  455.7 0.6 compare_reduce_fusion
  456.4 0.7 fusion.4
  457.0 9.8 %custom-call.9 = f32[1,1,128,128]{2,3,1,0:T(8,128)S(1)} custom-call(f32[1,1,128,128]{3,2,1,0:T(8,128)S(1)} %get-tuple-element.5), custom_call_target="InvertDiagBlocksLowerTriangular" | custom-call | tf_op jit(solution)/shard_map/vmap(jit(_solve_triangular))/triangular_solve | solution.py:10
  466.8 0.0 copy-done.2
  466.8 0.6 convolution_bitcast_fusion.1
  467.5 1.0 copy.7
  468.5 0.7 copy.8
  (1 shorter events, 0.0 us)
Async XLA Ops:
  7.2 27.9 %all-gather.2.cloned.1.call-start = ((), (), s32[]{:S(2)}) async-start(), calls=%async_computation.1 | async-start | bytes 2621440 | tf_op jit(solution)/shard_map/all_gather | solution.py:35
  7.9 139.9 %all-reduce.5.cloned.1.call-start = ((), (), s32[]{:S(2)}) async-start(), calls=%async_computation.2 | async-start | bytes 4194304 | tf_op jit(solution)/shard_map/psum | solution.py:36
  45.3 1.0 copy-start.1
  45.3 170.0 %all-reduce.7.cloned.1.call-start = ((), (), s32[]{:S(2)}) async-start(), calls=%async_computation.3 | async-start | bytes 4194304 | tf_op jit(solution)/shard_map/psum | solution.py:40
  164.5 163.6 %all-reduce.9.cloned.1.call-start = ((), (), s32[]{:S(2)}) async-start(), calls=%async_computation.4 | async-start | bytes 4194304 | tf_op jit(solution)/shard_map/psum | solution.py:43
  225.6 143.4 %reduce-scatter.2.cloned.1.call-start = ((), (), s32[]{:S(2)}) async-start(), calls=%async_computation.5 | async-start | bytes 2621440 | tf_op jit(solution)/shard_map/reduce_scatter | solution.py:44
  338.4 30.6 %copy-start = (f32[1024,512]{0,1:T(8,128)S(1)}, f32[1024,512]{0,1:T(8,128)}, u32[]{:S(2)}) copy-start(f32[1024,512]{0,1:T(8,128)} %all-reduce.7.cloned.1.call-done) | copy-start | bytes 6291460
  338.4 103.8 %all-reduce.11.cloned.1.call-start = ((), (), s32[]{:S(2)}) async-start(), calls=%async_computation.6 | async-start | bytes 131072 | tf_op jit(solution)/shard_map/psum | solution.py:48
  369.0 97.8 %copy-start.2 = (f32[1024,128]{0,1:T(8,128)S(1)}, f32[1024,128]{0,1:T(8,128)}, u32[]{:S(2)}) copy-start(f32[1024,128]{0,1:T(8,128)} %reduce-scatter.2.cloned.1.call-done) | copy-start | bytes 1572868
Sparse Core Ops, SparseCore 0:
  9.5 25.5 all-gather.1
  45.4 102.3 all-reduce.4
  164.6 50.6 all-reduce.6
  225.7 102.3 all-reduce.8
  338.5 30.4 reduce-scatter.1
  372.9 69.2 all-reduce.10
where the time goes:
time: 476 us
  waiting for transfers between devices  383 us (80%)
  matrix products  50.5 us (11%)
  other arithmetic  23.7 us (5%)
  between operations  14.2 us (3%)
    psum x1, waiting for transfers between devices, body(): coef_two = lax.psum(terms_two, 'rows')  102 us
    psum x1, waiting for transfers between devices, body(): coef_one = lax.psum(terms_one, 'rows')  101 us
    psum x1, waiting for transfers between devices, body(): gram = lax.psum(gram, 'rows')  70.6 us
    psum x1, waiting for transfers between devices, body(): first_whole = lax.psum(placed - expand(coef_one), 'cols')  50.6 us
    reduce_scatter x1, waiting for transfers between devices, body(): lax.psum_scatter(expand(coef_two), 'cols', scatter_dimension=1, tiled=True)  30.3 us
    all_gather x1, waiting for transfers between devices, body(): terms_one = project(lax.all_gather(block, 'cols', axis=1, tiled=True))  27.2 us
    dot_general x2, matrix products, expand(): jnp.dot(basis, coef, precision=highest, preferred_element_type=jnp.float32)  27 us
    dot_general x2, matrix products, project(): lax.dot_general(basis, piece, (((0,), (0,)), ((), ())), precision=highest...  20.4 us
  transfers between devices with their start and end apart: 6, of which 6 were waited for; matrix products, arithmetic and copies ran while one was open for 0% of the time, Pallas kernels for 0%

commit v1 on v0

--- a/solution.py
+++ b/solution.py
@@ -40,7 +40,9 @@
     first_whole = lax.psum(placed - expand(coef_one), "cols")
     terms_two = project(first_whole)
     first = lax.dynamic_slice_in_dim(first_whole, column_index * width, width, 1)
-    coef_two = lax.psum(terms_two, "rows")
+    coef_two = terms_two
+    for hop in (1, 2, 4):
+        coef_two = coef_two + lax.ppermute(coef_two, "rows", [(dev, dev ^ hop) for dev in range(8)])
     second = first - lax.psum_scatter(expand(coef_two), "cols", scatter_dimension=1, tiled=True)
     blocks = width // BLK
     pieces = second.reshape(local_rows, blocks, BLK)

time: 476 us -> 558 us (1.17)
  waiting for transfers between devices: 383 us -> 461 us
    ppermute x0 -> x3, waiting for transfers between devices: none -> 179 us  [body(): lax.ppermute(coef_two, 'rows', [(dev, dev ^ hop) for dev in range(8)])]
    psum x1 -> x0, waiting for transfers between devices: 102 us -> none  [body(): coef_two = lax.psum(terms_two, 'rows')]
  transfers between devices with their start and end apart: 6 -> 8, of which waited for: 6 -> 8; matrix products, arithmetic and copies ran while one was open for 0% -> 0% of each run, Pallas kernels for 0% -> 0%
where the time goes in v1:
time: 558 us
  waiting for transfers between devices  461 us (83%)
  matrix products  47.9 us (9%)
  other arithmetic  24.7 us (4%)
  between operations  13.9 us (2%)
  starting transfers between devices  6.16 us (1%)
    ppermute x3, waiting for transfers between devices, body(): lax.ppermute(coef_two, 'rows', [(dev, dev ^ hop) for dev in range(8)])  179 us
    psum x1, waiting for transfers between devices, body(): coef_one = lax.psum(terms_one, 'rows')  101 us
    psum x1, waiting for transfers between devices, body(): gram = lax.psum(gram, 'rows')  70.6 us
    psum x1, waiting for transfers between devices, body(): first_whole = lax.psum(placed - expand(coef_one), 'cols')  50.6 us
    reduce_scatter x1, waiting for transfers between devices, body(): lax.psum_scatter(expand(coef_two), 'cols', scatter_dimension=1, tiled=True)  31.5 us
    all_gather x1, waiting for transfers between devices, body(): terms_one = project(lax.all_gather(block, 'cols', axis=1, tiled=True))  27.2 us
    dot_general x2, matrix products, expand(): jnp.dot(basis, coef, precision=highest, preferred_element_type=jnp.float32)  24.9 us
    dot_general x2, matrix products, project(): lax.dot_general(basis, piece, (((0,), (0,)), ((), ())), precision=highest...  19.8 us
  transfers between devices with their start and end apart: 8, of which 8 were waited for; matrix products, arithmetic and copies ran while one was open for 0% of the time, Pallas kernels for 0%

profile of v1, /device:TPU:0, one launch (start us, length us, event | category | flops | bytes accessed | tf_op | source)
XLA Modules:
  0.0 557.5 jit_solution(7867512145712575013)
XLA Ops:
  7.2 0.0 all-gather.2.cloned.1.call-start
  7.2 0.7 all-gather.2.cloned.1.call-update
  7.9 0.0 all-reduce.4.cloned.1.call-start
  7.9 27.2 %all-gather.2.cloned.1.call-done = f32[1024,512]{1,0:T(8,128)} async-done(((f32[1024,128]{1,0:T(8,128)}), f32[1024,512]{1,0:T(8,128)}) %all-gather.2.cloned.1.call-update) | async-done | bytes 2097168 | tf_op jit(solution)/shard_map/all_gather | solution.py:35
  35.1 10.2 %convolution_multiply_fusion = f32[1024,512]{1,0:T(8,128)} fusion(f32[1024,1024]{1,0:T(8,128)} %param.2, f32[1024,512]{1,0:T(8,128)} %all-gather.2.cloned.1.call-done), kind=kOutput, calls=%fused_computation.5 | convolution fusion | flops 6442975232 | bytes 8388608 | tf_op jit(solution)/shard_map/dot_general | solution.py:22
  45.3 0.0 copy-start.2
  45.3 0.0 all-reduce.4.cloned.1.call-update
  45.3 0.0 all-reduce.6.cloned.1.call-start
  45.4 1.0 copy-done.2
  46.3 0.2 copy.4
  46.5 0.2 broadcast_in_dim.7
  46.8 0.1 constant_dynamic-update-slice_fusion
  46.8 100.9 %all-reduce.4.cloned.1.call-done = f32[1024,512]{1,0:T(8,128)} async-done(((f32[1024,512]{1,0:T(8,128)}), f32[1024,512]{1,0:T(8,128)}) %all-reduce.4.cloned.1.call-update) | async-done | bytes 2097168 | tf_op jit(solution)/shard_map/psum | solution.py:36
  147.8 16.7 %bitcast_subtract_fusion = f32[1024,512]{0,1:T(8,128)} fusion(f32[1024,512]{0,1:T(8,128)S(1)} %constant_dynamic-update-slice_fusion, f32[1024,512]{1,0:T(8,128)} %all-reduce.4.cloned.1.call-done, f32[1024,1024]{1,0:T(8,128)} %param.2), kind=kOutput, calls=%fused_computation | convolution fusion | flops 6442975232 | bytes 10485760 | tf_op jit(solution)/shard_map/dot_general | solution.py:33
  164.5 0.0 all-reduce.6.cloned.1.call-update
  164.5 0.2 reduce-scatter.2.cloned.1.call-start
  164.7 50.6 %all-reduce.6.cloned.1.call-done = f32[1024,512]{0,1:T(8,128)} async-done(((f32[1024,512]{0,1:T(8,128)}), f32[1024,512]{0,1:T(8,128)}) %all-reduce.6.cloned.1.call-update) | async-done | bytes 2097168 | tf_op jit(solution)/shard_map/psum | solution.py:40
  215.3 9.7 %multiply_bitcast_fusion = f32[1024,512]{0,1:T(8,128)S(1)} fusion(f32[1024,512]{0,1:T(8,128)} %all-reduce.6.cloned.1.call-done, f32[1024,1024]{1,0:T(8,128)} %param.2), kind=kOutput, calls=%fused_computation.3 | convolution fusion | flops 6442975232 | bytes 8388608 | tf_op jit(solution)/shard_map/dot_general | solution.py:22
  225.0 1.5 collective-permute-start
  226.5 45.7 %collective-permute-done = f32[1024,512]{0,1:T(8,128)S(1)} collective-permute-done((f32[1024,512]{0,1:T(8,128)S(1)}, f32[1024,512]{0,1:T(8,128)S(1)}, u32[]{:S(2)}, u32[]{:S(2)}) %collective-permute-start) | collective-permute-done | bytes 2097184 | tf_op jit(solution)/shard_map/ppermute | solution.py:45
  272.2 0.6 add.34
  272.7 0.0 copy-start
  272.7 1.5 collective-permute-start.1
  274.3 44.8 %collective-permute-done.1 = f32[1024,512]{0,1:T(8,128)S(1)} collective-permute-done((f32[1024,512]{0,1:T(8,128)S(1)}, f32[1024,512]{0,1:T(8,128)S(1)}, u32[]{:S(2)}, u32[]{:S(2)}) %collective-permute-start.1) | collective-permute-done | bytes 2097184 | tf_op jit(solution)/shard_map/ppermute | solution.py:45
  319.1 0.4 add.35
  319.5 2.5 collective-permute-start.2
  322.0 88.9 %collective-permute-done.2 = f32[1024,512]{0,1:T(8,128)S(1)} collective-permute-done((f32[1024,512]{0,1:T(8,128)S(1)}, f32[1024,512]{0,1:T(8,128)S(1)}, u32[]{:S(2)}, u32[]{:S(2)}) %collective-permute-start.2) | collective-permute-done | bytes 2097184 | tf_op jit(solution)/shard_map/ppermute | solution.py:45
  410.9 0.0 copy-done
  410.9 8.2 %fusion.2 = f32[1024,512]{0,1:T(8,128)} fusion(f32[1024,1024]{1,0:T(8,128)S(1)} %copy-done, f32[1024,512]{0,1:T(8,128)S(1)} %add.35, f32[1024,512]{0,1:T(8,128)S(1)} %collective-permute-done.2), kind=kOutput, calls=%fused_computation.4 | convolution fusion | flops 6442975232 | bytes 10485760 | tf_op jit(solution)/shard_map/dot_general | solution.py:33
  419.1 0.0 copy-start.1
  419.1 0.0 reduce-scatter.2.cloned.1.call-update
  419.1 0.3 all-reduce.8.cloned.1.call-start
  419.4 31.5 %reduce-scatter.2.cloned.1.call-done = f32[1024,128]{0,1:T(8,128)} async-done(((f32[1024,512]{0,1:T(8,128)}), f32[1024,128]{0,1:T(8,128)}) %reduce-scatter.2.cloned.1.call-update) | async-done | bytes 524304 | tf_op jit(solution)/shard_map/reduce_scatter | solution.py:46
  450.9 0.0 copy-done.1
  450.9 0.0 copy-start.3
  450.9 2.5 fusion.5
  453.4 0.0 all-reduce.8.cloned.1.call-update
  453.4 70.6 %all-reduce.8.cloned.1.call-done = f32[1,128,128]{1,2,0:T(8,128)} async-done(((f32[1,128,128]{1,2,0:T(8,128)}), f32[1,128,128]{1,2,0:T(8,128)}) %all-reduce.8.cloned.1.call-update) | async-done | bytes 65552 | tf_op jit(solution)/shard_map/psum | solution.py:50
  524.0 0.9 copy.6
  524.9 0.9 fusion.8
  525.8 11.7 %custom-call.8 = f32[1,128,128]{2,1,0:T(8,128)S(1)} custom-call(f32[1,128,128]{2,1,0:T(8,128)S(1)} %fusion.8), custom_call_target="Cholesky" | custom-call | tf_op jit(solution)/shard_map/jit(cholesky)/cholesky | solution.py:51
  537.5 0.6 compare_reduce_fusion
  538.2 0.7 fusion.9
  538.8 0.7 copy.8
  539.6 9.8 %custom-call.9 = f32[1,1,128,128]{2,3,1,0:T(8,128)S(1)} custom-call(f32[1,1,128,128]{3,2,1,0:T(8,128)S(1)} %get-tuple-element.5), custom_call_target="InvertDiagBlocksLowerTriangular" | custom-call | tf_op jit(solution)/shard_map/vmap(jit(_solve_triangular))/triangular_solve | solution.py:10
  549.4 0.0 copy-done.3
  549.4 0.6 convolution_bitcast_fusion
  550.0 1.0 copy.7
  (1 shorter events, 0.0 us)
Async XLA Ops:
  7.2 27.9 %all-gather.2.cloned.1.call-start = ((), (), s32[]{:S(2)}) async-start(), calls=%async_computation.1 | async-start | bytes 2621440 | tf_op jit(solution)/shard_map/all_gather | solution.py:35
  7.9 139.9 %all-reduce.4.cloned.1.call-start = ((), (), s32[]{:S(2)}) async-start(), calls=%async_computation.2 | async-start | bytes 4194304 | tf_op jit(solution)/shard_map/psum | solution.py:36
  45.3 1.0 copy-start.2
  45.3 170.0 %all-reduce.6.cloned.1.call-start = ((), (), s32[]{:S(2)}) async-start(), calls=%async_computation.3 | async-start | bytes 4194304 | tf_op jit(solution)/shard_map/psum | solution.py:40
  164.5 286.4 %reduce-scatter.2.cloned.1.call-start = ((), (), s32[]{:S(2)}) async-start(), calls=%async_computation.4 | async-start | bytes 2621440 | tf_op jit(solution)/shard_map/reduce_scatter | solution.py:46
  225.0 47.2 %collective-permute-start = (f32[1024,512]{0,1:T(8,128)S(1)}, f32[1024,512]{0,1:T(8,128)S(1)}, u32[]{:S(2)}, u32[]{:S(2)}) collective-permute-start(f32[1024,512]{0,1:T(8,128)S(1)} %multiply_bitcast_fusion), channel_id=1, source_target_pairs={{0,4},{4,0},{8,12},{12,8},{16,20},{20,16},{24,28},{28,24},{1,5},{5... | collective-permute-start | bytes 6291464 | tf_op jit(solution)/shard_map/ppermute | solution.py:45
  272.7 138.1 %copy-start = (f32[1024,1024]{1,0:T(8,128)S(1)}, f32[1024,1024]{1,0:T(8,128)}, u32[]{:S(2)}) copy-start(f32[1024,1024]{1,0:T(8,128)} %param.2) | copy-start | bytes 12582916
  272.7 46.3 %collective-permute-start.1 = (f32[1024,512]{0,1:T(8,128)S(1)}, f32[1024,512]{0,1:T(8,128)S(1)}, u32[]{:S(2)}, u32[]{:S(2)}) collective-permute-start(f32[1024,512]{0,1:T(8,128)S(1)} %add.34), channel_id=1, source_target_pairs={{0,8},{4,12},{8,0},{12,4},{16,24},{20,28},{24,16},{28,20},{1,9},{5... | collective-permute-start | bytes 6291464 | tf_op jit(solution)/shard_map/ppermute | solution.py:45
  319.5 91.3 %collective-permute-start.2 = (f32[1024,512]{0,1:T(8,128)S(1)}, f32[1024,512]{0,1:T(8,128)S(1)}, u32[]{:S(2)}, u32[]{:S(2)}) collective-permute-start(f32[1024,512]{0,1:T(8,128)S(1)} %add.35), channel_id=1, source_target_pairs={{0,16},{4,20},{8,24},{12,28},{16,0},{20,4},{24,8},{28,12},{1,17},{... | collective-permute-start | bytes 6291464 | tf_op jit(solution)/shard_map/ppermute | solution.py:45
  419.1 31.8 %copy-start.1 = (f32[1024,512]{0,1:T(8,128)S(1)}, f32[1024,512]{0,1:T(8,128)}, u32[]{:S(2)}) copy-start(f32[1024,512]{0,1:T(8,128)} %all-reduce.6.cloned.1.call-done) | copy-start | bytes 6291460
  419.1 104.9 %all-reduce.8.cloned.1.call-start = ((), (), s32[]{:S(2)}) async-start(), calls=%async_computation.5 | async-start | bytes 131072 | tf_op jit(solution)/shard_map/psum | solution.py:50
  450.9 98.5 %copy-start.3 = (f32[1024,128]{0,1:T(8,128)S(1)}, f32[1024,128]{0,1:T(8,128)}, u32[]{:S(2)}) copy-start(f32[1024,128]{0,1:T(8,128)} %reduce-scatter.2.cloned.1.call-done) | copy-start | bytes 1572868
Sparse Core Ops, SparseCore 0:
  9.5 25.5 all-gather.1
  45.4 102.3 all-reduce.3
  164.6 50.6 all-reduce.5
  419.2 31.6 reduce-scatter.1
  454.7 69.2 all-reduce.7
